TPU v7x, 8 devices: a whole 2x2x1 slice. The times are simulated.
8 devices in a mesh: sys: 1 (over z), gx: 2 (over y), gy: 2 (over x), gz: 2 (over core).
Axes of the slice: x: 2, y: 2, z: 1, core: 2. Of those that a mesh axis runs over, the one named last changes fastest.
Arguments:
- source: float32 [96, 128, 128], P(('sys', 'gx'), 'gy', 'gz')
- initial: float32 [96, 128, 128], P(('sys', 'gx'), 'gy', 'gz')
- velocity: float32 [3, 96, 128, 128], P(None, ('sys', 'gx'), 'gy', 'gz')
- damping: float32 [2, 10], P('sys')
Outputs:
- output 1: float32 [96, 128, 128], P(('sys', 'gx'), 'gy', 'gz')
- output 2: float32 [2, 11], P('sys')
All inputs are finite; a program needn't handle non-finite values.
Results may differ from a plain program's by a relative error of at most 0.001.
Values sent between devices are 32-bit elements.
A program may use at most 1 GiB of HBM per device.

v0:
```python
import math
import jax
import jax.numpy as jnp
from jax import lax
from jax.sharding import PartitionSpec as P

SWEEPS = 3
GRID_AXES = ('gx', 'gy', 'gz')


def zero_planes(field):
    plane_pairs = []
    for axis_pos in range(3):
        plane_shape = list(field.shape)
        plane_shape[axis_pos] = 1
        empty_plane = jnp.zeros(tuple(plane_shape), field.dtype)
        plane_pairs.append((empty_plane, empty_plane))
    return plane_pairs


def exchange(field, axis_sizes):
    plane_pairs = []
    for axis_pos in range(3):
        extent = field.shape[axis_pos]
        first_plane = jnp.split(field, [1], axis=axis_pos)[0]
        last_plane = jnp.split(field, [extent - 1], axis=axis_pos)[1]
        member_count = axis_sizes[axis_pos]
        if member_count == 1:
            plane_pairs.append((jnp.zeros_like(last_plane), jnp.zeros_like(first_plane)))
        else:
            to_next = [(member, member + 1) for member in range(member_count - 1)]
            to_prev = [(member + 1, member) for member in range(member_count - 1)]
            low_plane = lax.ppermute(last_plane, GRID_AXES[axis_pos], to_next)
            high_plane = lax.ppermute(first_plane, GRID_AXES[axis_pos], to_prev)
            plane_pairs.append((low_plane, high_plane))
    return plane_pairs


def stencil(field, velocity, plane_pairs):
    result = 6.0 * field
    for axis_pos in range(3):
        extent = field.shape[axis_pos]
        low_plane, high_plane = plane_pairs[axis_pos]
        ahead_val = jnp.concatenate([jnp.split(field, [1], axis=axis_pos)[1], high_plane], axis=axis_pos)
        behind_val = jnp.concatenate([low_plane, jnp.split(field, [extent - 1], axis=axis_pos)[0]], axis=axis_pos)
        result = result - ahead_val - behind_val + 0.5 * velocity[axis_pos] * (ahead_val - behind_val)
    return result


def precondition(vector, velocity, relax_w):
    step_scale = relax_w / 6.0
    approx = step_scale * vector
    local_planes = zero_planes(vector)
    for sweep_id in range(SWEEPS - 1):
        approx = approx + step_scale * (vector - stencil(approx, velocity, local_planes))
    return approx


def givens_solve(hessen, beta_zero):
    col_count = hessen.shape[1]
    rot_rows = hessen
    rhs_vec = jnp.zeros((col_count + 1,), jnp.float32).at[0].set(beta_zero)
    sine_list = []
    for col_id in range(col_count):
        diag_val = rot_rows[col_id, col_id]
        below_val = rot_rows[col_id + 1, col_id]
        radius = jnp.sqrt(diag_val * diag_val + below_val * below_val)
        cosine = diag_val / radius
        sine_val = below_val / radius
        upper_row = cosine * rot_rows[col_id] + sine_val * rot_rows[col_id + 1]
        lower_row = cosine * rot_rows[col_id + 1] - sine_val * rot_rows[col_id]
        rot_rows = rot_rows.at[col_id].set(upper_row).at[col_id + 1].set(lower_row)
        lead_val = rhs_vec[col_id]
        rhs_vec = rhs_vec.at[col_id].set(cosine * lead_val).at[col_id + 1].set(-sine_val * lead_val)
        sine_list.append(jnp.abs(sine_val))
    coeffs = jnp.zeros((col_count,), jnp.float32)
    for row_id in reversed(range(col_count)):
        remainder = rhs_vec[row_id] - jnp.sum(rot_rows[row_id] * coeffs)
        coeffs = coeffs.at[row_id].set(remainder / rot_rows[row_id, row_id])
    factors = jnp.concatenate([jnp.ones((1,), jnp.float32), jnp.stack(sine_list)])
    return coeffs, beta_zero * jnp.cumprod(factors)


def solution(mesh):
    axis_sizes = tuple(mesh.shape[axis_label] for axis_label in GRID_AXES)
    grid_spec = P(('sys', 'gx'), 'gy', 'gz')
    vel_spec = P(None, ('sys', 'gx'), 'gy', 'gz')
    table_spec = P('sys', None)
    full_prec = lax.Precision.HIGHEST

    def local_solve(source, initial, velocity, damping):
        cycles, restart = damping.shape
        out_scale = 1.0 / math.sqrt(source.size * axis_sizes[0] * axis_sizes[1] * axis_sizes[2])
        current = initial
        rows_out = []
        for cycle_id in range(cycles):
            residual = source - stencil(current, velocity, exchange(current, axis_sizes))
            beta_zero = jnp.sqrt(lax.psum(jnp.sum(residual * residual), GRID_AXES))
            basis = jnp.zeros((restart + 1,) + source.shape, jnp.float32).at[0].set(residual / beta_zero)
            search = jnp.zeros((restart,) + source.shape, jnp.float32)
            hessen = jnp.zeros((restart + 1, restart), jnp.float32)
            for col_id in range(restart):
                precond_vec = precondition(basis[col_id], velocity, damping[cycle_id, col_id])
                search = search.at[col_id].set(precond_vec)
                work_vec = stencil(precond_vec, velocity, exchange(precond_vec, axis_sizes))
                active = basis[:col_id + 1]
                proj_one = lax.psum(jnp.einsum('kabc,abc->k', active, work_vec, preferred_element_type=jnp.float32, precision=full_prec), GRID_AXES)
                work_vec = work_vec - jnp.einsum('k,kabc->abc', proj_one, active, preferred_element_type=jnp.float32, precision=full_prec)
                proj_two = lax.psum(jnp.einsum('kabc,abc->k', active, work_vec, preferred_element_type=jnp.float32, precision=full_prec), GRID_AXES)
                work_vec = work_vec - jnp.einsum('k,kabc->abc', proj_two, active, preferred_element_type=jnp.float32, precision=full_prec)
                norm_w = jnp.sqrt(lax.psum(jnp.sum(work_vec * work_vec), GRID_AXES))
                basis = basis.at[col_id + 1].set(work_vec / norm_w)
                hessen = hessen.at[:col_id + 1, col_id].set(proj_one + proj_two).at[col_id + 1, col_id].set(norm_w)
            coeffs, estimates = givens_solve(hessen, beta_zero)
            current = current + jnp.einsum('k,kabc->abc', coeffs, search, preferred_element_type=jnp.float32, precision=full_prec)
            rows_out.append(estimates * out_scale)
        return current, jnp.stack(rows_out)

    return jax.shard_map(local_solve, mesh=mesh, in_specs=(grid_spec, grid_spec, vel_spec, table_spec), out_specs=(grid_spec, table_spec), check_vma=False)
```

profile of v0, /device:TPU:0, one launch (start us, length us, event | category | flops | bytes accessed | tf_op | source)
XLA Modules:
  0.0 5734.7 jit_solution(1726244418057624259)
XLA Ops:
  327.8 40.4 fusion.339
  410.7 40.3 fusion.342
  587.2 68.5 %fusion.199 = f32[3]{0:T(128)S(1)} fusion(f32[48,64,64,1]{2,0,1,3:T(8,128)S(1)} %bitcast.1492, f32[3,48,64,64]{3,1,2,0:T(8,128)} %slice.3981), kind=kOutput, calls=%fused_computation.482 | convolution fusion | flops 7077888 | bytes 3145740 | tf_op jit(solution)/shard_map/kabc,abc->k/dot_general | solution.py:107
  699.6 68.3 %fusion.204 = f32[3]{0:T(128)S(1)} fusion(f32[48,64,64,1]{2,0,1,3:T(8,128)S(1)} %fusion.364, f32[3,48,64,64]{3,1,2,0:T(8,128)} %slice.3981), kind=kOutput, calls=%fused_computation.483 | convolution fusion | flops 7077888 | bytes 3145740 | tf_op jit(solution)/shard_map/kabc,abc->k/dot_general | solution.py:109
  812.2 25.1 psum.443
  908.1 73.8 %fusion.179 = f32[4]{0:T(128)S(1)} fusion(f32[48,64,64,1]{2,0,1,3:T(8,128)S(1)} %bitcast.1493, f32[4,48,64,64]{3,1,2,0:T(8,128)} %slice.3982), kind=kOutput, calls=%fused_computation.478 | convolution fusion | flops 9437184 | bytes 3932176 | tf_op jit(solution)/shard_map/kabc,abc->k/dot_general | solution.py:107
  1027.2 73.6 %fusion.184 = f32[4]{0:T(128)S(1)} fusion(f32[48,64,64,1]{2,0,1,3:T(8,128)S(1)} %fusion.365, f32[4,48,64,64]{3,1,2,0:T(8,128)} %slice.3982), kind=kOutput, calls=%fused_computation.479 | convolution fusion | flops 9437184 | bytes 3932176 | tf_op jit(solution)/shard_map/kabc,abc->k/dot_general | solution.py:109
  1244.1 32.5 fusion.279
  1322.3 31.9 fusion.284
  1499.3 33.5 fusion.259
  1579.9 32.9 fusion.264
  1660.9 25.2 psum.452
  1760.2 34.4 fusion.239
  1842.1 34.2 fusion.244
  2025.4 28.1 fusion.219
  2102.0 34.9 fusion.224
  2287.9 35.7 fusion.319
  2373.6 34.5 fusion.324
  2458.5 25.2 psum.461
  2562.1 35.7 fusion.299
  2622.4 27.4 fusion.28
  2651.9 42.2 fusion.304
  2718.2 27.4 fusion.24
  2856.2 27.4 fusion.34
  3082.2 25.3 psum.468
  3175.5 40.4 fusion.345
  3258.4 40.3 fusion.348
  3340.0 25.1 psum.471
  3434.6 68.5 %fusion.209 = f32[3]{0:T(128)S(1)} fusion(f32[48,64,64,1]{2,0,1,3:T(8,128)S(1)} %bitcast.1490, f32[3,48,64,64]{3,1,2,0:T(8,128)} %slice.4038), kind=kOutput, calls=%fused_computation.484 | convolution fusion | flops 7077888 | bytes 3145740 | tf_op jit(solution)/shard_map/kabc,abc->k/dot_general | solution.py:107
  3547.0 68.3 %fusion.214 = f32[3]{0:T(128)S(1)} fusion(f32[48,64,64,1]{2,0,1,3:T(8,128)S(1)} %fusion.373, f32[3,48,64,64]{3,1,2,0:T(8,128)} %slice.4038), kind=kOutput, calls=%fused_computation.485 | convolution fusion | flops 7077888 | bytes 3145740 | tf_op jit(solution)/shard_map/kabc,abc->k/dot_general | solution.py:109
  3755.8 73.8 %fusion.189 = f32[4]{0:T(128)S(1)} fusion(f32[48,64,64,1]{2,0,1,3:T(8,128)S(1)} %bitcast.1491, f32[4,48,64,64]{3,1,2,0:T(8,128)} %slice.4039), kind=kOutput, calls=%fused_computation.480 | convolution fusion | flops 9437184 | bytes 3932176 | tf_op jit(solution)/shard_map/kabc,abc->k/dot_general | solution.py:107
  3874.9 73.6 %fusion.194 = f32[4]{0:T(128)S(1)} fusion(f32[48,64,64,1]{2,0,1,3:T(8,128)S(1)} %fusion.374, f32[4,48,64,64]{3,1,2,0:T(8,128)} %slice.4039), kind=kOutput, calls=%fused_computation.481 | convolution fusion | flops 9437184 | bytes 3932176 | tf_op jit(solution)/shard_map/kabc,abc->k/dot_general | solution.py:109
  4091.6 32.5 fusion.289
  4169.8 31.9 fusion.294
  4346.9 33.5 fusion.269
  4427.4 32.9 fusion.274
  4508.5 25.2 psum.483
  4607.8 34.4 fusion.249
  4689.7 34.2 fusion.254
  4873.3 28.1 fusion.229
  4949.9 34.9 fusion.234
  5135.9 35.7 fusion.329
  5221.6 34.5 fusion.334
  5410.1 35.7 fusion.309
  5470.5 27.4 fusion.20
  5498.8 42.2 fusion.314
  5565.1 27.3 fusion.16
  5703.9 27.4 fusion.32
  (1469 shorter events, 3719.2 us)
Async XLA Ops:
  6.4 28.2 collective-permute-start.4
  8.2 60.1 %collective-permute-start.5 = (f32[48,64,1]{1,0,2:T(8,128)S(1)}, f32[48,64,1]{1,0,2:T(8,128)S(1)}, u32[]{:S(2)}, u32[]{:S(2)}) collective-permute-start(f32[48,64,1]{1,0,2:T(8,128)S(1)} %copy.319), channel_id=1, source_target_pairs={{0,1},{2,3},{4,5},{6,7}} | collective-permute-start | bytes 36872 | tf_op jit(solution)/shard_map/ppermute | solution.py:33
  11.2 58.8 %collective-permute-start = (f32[1,64,64]{2,0,1:T(1,128)S(1)}, f32[1,64,64]{2,0,1:T(1,128)S(1)}, u32[]{:S(2)}, u32[]{:S(2)}) collective-permute-start(f32[1,64,64]{2,0,1:T(1,128)S(1)} %bitcast.1499), channel_id=1, source_target_pairs={{4,0},{5,1},{6,2},{7,3}} | collective-permute-start | bytes 49160 | tf_op jit(solution)/shard_map/ppermute | solution.py:34
  12.5 57.5 %collective-permute-start.1 = (f32[1,64,64]{2,0,1:T(1,128)S(1)}, f32[1,64,64]{2,0,1:T(1,128)S(1)}, u32[]{:S(2)}, u32[]{:S(2)}) collective-permute-start(f32[1,64,64]{2,0,1:T(1,128)S(1)} %bitcast.1498), channel_id=1, source_target_pairs={{0,4},{1,5},{2,6},{3,7}} | collective-permute-start | bytes 49160 | tf_op jit(solution)/shard_map/ppermute | solution.py:33
  17.9 52.1 collective-permute-start.2
  34.6 35.4 collective-permute-start.3
  134.4 28.1 collective-permute-start.11
  137.5 26.9 collective-permute-start.6
  138.8 25.6 collective-permute-start.7
  871.3 26.3 collective-permute-start.29
  1206.0 27.6 collective-permute-start.35
  1209.0 26.4 collective-permute-start.30
  1460.1 28.7 collective-permute-start.41
  1463.1 27.5 collective-permute-start.36
  1464.4 26.2 collective-permute-start.37
  1720.0 29.7 collective-permute-start.47
  1723.0 28.4 collective-permute-start.42
  1724.3 27.1 collective-permute-start.43
  1984.1 30.3 collective-permute-start.53
  1987.2 29.1 collective-permute-start.48
  1988.5 27.8 collective-permute-start.49
  2245.3 31.2 collective-permute-start.59
  2248.3 30.0 collective-permute-start.54
  2249.6 28.7 collective-permute-start.55
  2517.5 32.4 collective-permute-start.65
  2520.5 31.2 collective-permute-start.60
  2521.8 29.9 collective-permute-start.61
  2982.0 28.0 collective-permute-start.77
  2985.0 26.7 collective-permute-start.72
  3719.0 26.3 collective-permute-start.95
  4053.4 27.6 collective-permute-start.101
  4056.4 26.4 collective-permute-start.96
  4307.7 28.6 collective-permute-start.107
  4310.7 27.4 collective-permute-start.102
  4312.0 26.1 collective-permute-start.103
  4567.5 29.7 collective-permute-start.113
  4570.6 28.4 collective-permute-start.108
  4571.9 27.1 collective-permute-start.109
  4831.9 30.5 collective-permute-start.119
  4834.9 29.3 collective-permute-start.114
  4836.2 28.0 collective-permute-start.115
  5093.4 31.1 collective-permute-start.125
  5096.4 29.9 collective-permute-start.120
  5097.7 28.6 collective-permute-start.121
  5365.4 32.6 collective-permute-start.131
  5368.4 31.4 collective-permute-start.126
  5369.7 30.1 collective-permute-start.127
  5374.3 25.5 collective-permute-start.128
  (259 other events, 4136.4 us)
where the time goes:
time: 5770 us; the launch traced here: 5730 us
  matrix products  2370 us (41%)
  blocking collectives  1450 us (25%)
  local copies, waits for them, and re-layouts  736 us (13%)
  other arithmetic  677 us (12%)
  starting transfers between devices  358 us (6%)
  between operations  149 us (3%)
    dot_general x36, matrix products, local_solve(): jnp.einsum('kabc,abc->k', active, work_vec, preferred_element_type=jnp.fl...  1550 us
    psum x40, blocking collectives, local_solve(): lax.psum(jnp.einsum('kabc,abc->k', active, work_vec, preferred_element_ty...  903 us
    psum x20, blocking collectives, local_solve(): norm_w = jnp.sqrt(lax.psum(jnp.sum(work_vec * work_vec), GRID_AXES))  500 us
    dot_general x18, matrix products, local_solve(): jnp.einsum('k,kabc->abc', proj_two, active, preferred_element_type=jnp.fl...  380 us
    dot_general x18, matrix products, local_solve(): jnp.einsum('k,kabc->abc', proj_one, active, preferred_element_type=jnp.fl...  380 us
    ppermute x66, starting transfers between devices, exchange(): low_plane = lax.ppermute(last_plane, GRID_AXES[axis_pos], to_next)  269 us
    split x186, local copies, waits for them, and re-layouts, stencil(): jnp.split(field, [1], axis=axis_pos)[1]  202 us
    add x18, other arithmetic, stencil(): result - ahead_val - behind_val  158 us
  transfers between devices with their start and end apart: 132, of which 0 were waited for; matrix products, arithmetic and copies ran while one was open for 7% of the time, Pallas kernels for 0%

commit v1 on v0

v1 whole, which is shorter than its diff:
```python
import math
import jax
import jax.numpy as jnp
from jax import lax
from jax.experimental import pallas as pl
from jax.experimental.pallas import tpu as pltpu
from jax.sharding import PartitionSpec as P

MESH = pl.DeviceIdType.MESH
RESTART = 10
CYCLES = 2
NP = 24
LO, HI, ROWS = 8, 72, 80
XG, YG, ZG = slice(0, 32), slice(32, 56), slice(56, 120)
GROWS = 120
UA, UB, UD, UI, UP, UR, UG = 2, 2, 2, 2, 2, 2, 1


def planes(unroll, body, carry=()):
    if unroll == NP:
        for p in range(1, NP + 1):
            carry = body(p, carry)
        return carry

    def trip(t, carry):
        for i in range(unroll):
            carry = body(t * unroll + (i + 1), carry)
        return carry
    return lax.fori_loop(0, NP // unroll, trip, carry)


def groups(fn):
    def trip(t, carry):
        for i in range(UG):
            fn(pl.ds(pl.multiple_of((t * UG + i) * 8, 8), 8))
        return carry
    lax.fori_loop(0, GROWS // 8 // UG, trip, 0)


def kernel(src_ref, ini_ref, vel_ref, damp_ref, out_ref, res_ref,
           U, Z, UC, ZC, T1, T2, W, X, SRC, CPZ, CMZ, HVX, HVY, CGZ,
           GU, RB, SB, GZ, GX, SS, ACC, GM, RM, SIG, EC, CS, SN, GV, YY, RES, MISC,
           s_send, s_recv, h_send, h_recv, x_recv):
    f32 = jnp.float32
    gx, gy, gz = lax.axis_index('gx'), lax.axis_index('gy'), lax.axis_index('gz')
    peers = {}
    for p in range(1, 8):
        a, b, c = p // 4, (p // 2) % 2, p % 2
        peers[p] = {'gx': 1 - gx if a else gx, 'gy': 1 - gy if b else gy, 'gz': 1 - gz if c else gz}
    side = {0: 4, 1: 2, 2: 1}

    bar = pltpu.get_barrier_semaphore()
    for p in range(1, 8):
        pl.semaphore_signal(bar, inc=1, device_id=peers[p], device_id_type=MESH)

    lane = lax.broadcasted_iota(jnp.int32, (64, 128), 1)
    lane8 = lane[0:8]
    left = lane < 64
    zlane = jnp.where(left, lane, lane - 64)
    zero64 = jnp.zeros((64, 128), f32)
    zero8 = jnp.zeros((8, 128), f32)
    hi_x = (1 - gx).astype(f32)
    hi_y = (1 - gy).astype(f32)
    l0 = 63 * (1 - gz)
    sx_lo, sx_hi = 64 * (1 - gx), 64 * gx
    y_send = HI - 1 - 63 * gy
    y_pad = HI - 65 * gy

    def seams(V, ghost=None):
        a = pltpu.roll(V[NP, LO:HI, :], 64, 1)
        b = pltpu.roll(V[1, LO:HI, :], 64, 1)
        if ghost is None:
            V[0, LO:HI, :] = jnp.where(left, 0.0, a)
            V[NP + 1, LO:HI, :] = jnp.where(left, b, 0.0)
        else:
            V[0, LO:HI, :] = jnp.where(left, ghost * (1.0 - hi_x), a)
            V[NP + 1, LO:HI, :] = jnp.where(left, b, ghost * hi_x)

    def stencil(V, p):
        u = V[p, LO:HI, :]
        yp, ym = V[p, LO + 1:HI + 1, :], V[p, LO - 1:HI - 1, :]
        xp, xm = V[p + 1, LO:HI, :], V[p - 1, LO:HI, :]
        n = CPZ[p - 1] * pltpu.roll(u, 127, 1) + CMZ[p - 1] * pltpu.roll(u, 1, 1)
        n = n + (xp + xm) - HVX[p - 1] * (xp - xm)
        n = n + (yp + ym) - HVY[p - 1] * (yp - ym)
        return u, 6.0 * u - n

    def ghost_z(cz, p):
        shift = (l0 - (p - 1) + 128) % 128
        return CGZ[p - 1] * pltpu.roll(cz, shift, 1)

    def fill_ghosts(V, rec):
        g = rec[XG, :]
        gfull = jnp.concatenate([pltpu.roll(g, sx_lo, 1), pltpu.roll(g, sx_hi, 1)], axis=0)
        seams(V, gfull)

        def row(p, c):
            V[p, pl.ds(y_pad, 1), :] = rec[pl.ds(p + 31, 1), :]
            return c
        planes(UP, row)

    def pack(V, q):
        pd = NP - 23 * gx
        plane = V[pd, LO:HI, :]
        a = pltpu.roll(plane[0:32], sx_lo, 1)
        b = pltpu.roll(plane[32:64], sx_hi, 1)
        SB[q, XG, :] = jnp.where(left[0:32], a, b)

        def row(p, acc):
            SB[q, pl.ds(p + 31, 1), :] = V[p, pl.ds(y_send, 1), :]
            shift = (p - 1 - l0 + 128) % 128
            return jnp.where(zlane == p - 1, pltpu.roll(V[p, LO:HI, :], shift, 1), acc)
        SB[q, ZG, :] = planes(UP, row, zero64)

    def halo(q, dst, sem):
        out = []
        for ax, rows in ((0, XG), (1, YG), (2, ZG)):
            out.append(pltpu.make_async_remote_copy(
                src_ref=SB.at[q, rows, :], dst_ref=dst.at[rows, :],
                send_sem=h_send.at[q, ax], recv_sem=sem.at[ax],
                device_id=peers[side[ax]], device_id_type=MESH))
        return out

    def sync_copies(par):
        return [pltpu.make_async_remote_copy(
            src_ref=SS.at[par, pl.ds(0, 1), :], dst_ref=SS.at[par, pl.ds(p, 1), :],
            send_sem=s_send.at[p], recv_sem=s_recv.at[par, p],
            device_id=peers[p], device_id_type=MESH) for p in range(1, 8)]

    def sync_start(par, items):
        row = zero8
        for idx, acc in items:
            row = jnp.where(lane8 == idx, jnp.sum(acc, axis=1, keepdims=True), row)
        row = row + pltpu.roll(row, 4, 0)
        row = row + pltpu.roll(row, 2, 0)
        row = row + pltpu.roll(row, 1, 0)
        SS[par, 0:1, :] = row[0:1]
        for cp in sync_copies(par):
            cp.start()

    def sync_wait(par):
        for cp in sync_copies(par):
            cp.wait_recv()
        for cp in sync_copies(par):
            cp.wait_send()
        tot = SS[par]
        tot = tot + pltpu.roll(tot, 4, 0)
        tot = tot + pltpu.roll(tot, 2, 0)
        return tot + pltpu.roll(tot, 1, 0)

    def bc(tot, k):
        return jnp.broadcast_to(tot[:, k:k + 1], (8, 128))

    def fold(x):
        return jnp.sum(x.reshape(8, 8, 128), axis=0)

    def wide(e):
        return jnp.concatenate([e] * 8, axis=0)

    def packed(lo, hi):
        return jnp.concatenate([lo, hi], axis=1)

    @pl.loop(0, NP + 2)
    def _(p):
        for V in (UC, ZC, T1, W, X):
            V[p, 0:LO, :] = zero8
            V[p, HI:ROWS, :] = zero8

    @pl.loop(0, NP)
    def _(i):
        X[i + 1, LO:HI, :] = packed(ini_ref[i], ini_ref[i + NP])
        SRC[i] = packed(src_ref[i], src_ref[i + NP])
        HVX[i] = 0.5 * packed(vel_ref[0, i], vel_ref[0, i + NP])
        HVY[i] = 0.5 * packed(vel_ref[1, i], vel_ref[1, i + NP])
        hz = 0.5 * packed(vel_ref[2, i], vel_ref[2, i + NP])
        first, last = zlane == 0, zlane == 63
        CPZ[i] = jnp.where(last, 0.0, 1.0 - hz)
        CMZ[i] = jnp.where(first, 0.0, 1.0 + hz)
        hi_z = (1 - gz).astype(f32)
        CGZ[i] = jnp.where(last, hi_z * (1.0 - hz), jnp.where(first, (1.0 - hi_z) * (1.0 + hz), 0.0))

    pack(X, 0)
    pl.semaphore_wait(bar, 7)
    cps = halo(0, GX, x_recv)
    for cp in cps:
        cp.start()
    for cp in cps:
        cp.wait()

    def residual(scale):
        fill_ghosts(X, GX)
        cz = GX[ZG, :]

        def one(p, acc):
            _, ax = stencil(X, p)
            r = SRC[p - 1] - (ax - ghost_z(cz, p))
            if scale is not None:
                r = r * wide(scale)
                U[0, p - 1] = r
            UC[p, LO:HI, :] = r
            return acc + fold(r * r)
        acc = planes(UR, one, zero8)
        seams(UC)
        return acc

    def block_apply(V, O, unroll):
        def one(p, c):
            _, t = stencil(V, p)
            O[p, LO:HI, :] = t
            return c
        planes(unroll, one)

    acc0 = residual(None)
    sync_start(0, [(16, acc0)])
    started = []
    pack(UC, 0)
    started += halo(0, GU.at[0, 0], h_recv.at[1, 0])
    for cp in started[0:3]:
        cp.start()
    block_apply(UC, T1, UR)
    seams(T1)
    pack(T1, 1)
    started += halo(1, GU.at[0, 1], h_recv.at[1, 1])
    for cp in started[3:6]:
        cp.start()
    block_apply(T1, T2, UR)
    pack(T2, 2)
    started += halo(2, GU.at[0, 2], h_recv.at[1, 2])
    for cp in started[6:9]:
        cp.start()
    tot = sync_wait(0)
    beta0 = jnp.sqrt(bc(tot, 16))
    inv0 = 1.0 / beta0
    MISC[0] = beta0
    MISC[1] = inv0
    ACC[0] = acc0 * inv0 * inv0

    def rescale(p, c):
        r = UC[p, LO:HI, :] * wide(inv0)
        UC[p, LO:HI, :] = r
        U[0, p - 1] = r
        return c
    planes(UP, rescale)
    seams(UC)
    for cp in started:
        cp.wait()

    def rescale_ghost(rows):
        for q in range(3):
            GU[0, q, rows, :] = GU[0, q, rows, :] * inv0
    groups(rescale_ghost)

    def givens(m, sub):
        h = [RM[i, m] for i in range(m + 1)]
        for i in range(m):
            cs, sn = CS[i], SN[i]
            h[i], h[i + 1] = cs * h[i] + sn * h[i + 1], cs * h[i + 1] - sn * h[i]
        d = h[m]
        rad = jnp.sqrt(d * d + sub * sub)
        cs, sn = d / rad, sub / rad
        CS[m] = cs
        SN[m] = sn
        h[m] = cs * d + sn * sub
        for i in range(m + 1):
            RM[i, m] = h[i]
        g = GV[m]
        GV[m] = cs * g
        GV[m + 1] = -sn * g
        est = MISC[4] * jnp.abs(sn)
        MISC[4] = est
        return est

    out_scale = 1.0 / math.sqrt(1572864.0)

    @pl.loop(0, CYCLES)
    def _(c):
        @pl.loop(0, RESTART)
        def _(j):
            step = c * RESTART + j
            par = (step + 1) % 2
            hpar = step % 2
            s = damp_ref[c, j] / 6.0
            a0, a1, a2 = 3.0 * s, 3.0 * s * s, s * s * s

            block_apply(UC, T1, UA)
            seams(T1)

            def precond(p, cy):
                t1, t2 = stencil(T1, p)
                z = a0 * UC[p, LO:HI, :] - a1 * t1 + a2 * t2
                ZC[p, LO:HI, :] = z
                Z[j, p - 1] = z
                return cy
            planes(UB, precond)

            for k in range(1, RESTART):
                @pl.when(j == k)
                def _():
                    for cp in [x for q in range(3) for x in halo(q, RB.at[c, k - 1, q], h_recv.at[1 - hpar, q])]:
                        cp.wait_recv()
                    ec = [EC[i] for i in range(k + 1)]

                    def ghost_u(rows):
                        for q in range(3):
                            g = ec[k] * RB[c, k - 1, q, rows, :]
                            for i in range(k):
                                g = g - ec[i] * GU[i, q, rows, :]
                            GU[k, q, rows, :] = g
                    groups(ghost_u)

            def ghost_of_z(rows):
                GZ[j, rows, :] = a0 * GU[j, 0, rows, :] - a1 * GU[j, 1, rows, :] + a2 * GU[j, 2, rows, :]
            groups(ghost_of_z)
            fill_ghosts(ZC, GZ.at[j])

            for k in range(RESTART):
                @pl.when(j == k)
                def _():
                    cz = GZ[k, ZG, :]

                    def one(p, accs):
                        accs = list(accs)
                        _, az = stencil(ZC, p)
                        w = az - ghost_z(cz, p)
                        W[p, LO:HI, :] = w
                        for i in range(k + 1):
                            accs[i] = accs[i] + fold(U[i, p - 1] * w)
                        if k == 0 or k == RESTART - 1:
                            accs[k + 1] = accs[k + 1] + fold(w * w)
                        return tuple(accs)
                    accs = planes(UD, one, (zero8,) * (k + 2))
                    accw = accs[k + 1]
                    items = [(i, accs[i]) for i in range(k + 1)] + [(16 + i, ACC[i]) for i in range(k + 1)]
                    if k == 0 or k == RESTART - 1:
                        items.append((32, accw))
                    sync_start(par, items)

            @pl.when(step < CYCLES * RESTART - 1)
            def _():
                seams(W)
                pack(W, 0)
                for cp in halo(0, RB.at[c, j, 0], h_recv.at[hpar, 0]):
                    cp.start()
                block_apply(W, T1, UI)
                seams(T1)
                pack(T1, 1)
                for cp in halo(1, RB.at[c, j, 1], h_recv.at[hpar, 1]):
                    cp.start()
                block_apply(T1, T2, UI)
                pack(T2, 2)
                for cp in halo(2, RB.at[c, j, 2], h_recv.at[hpar, 2]):
                    cp.start()

            tot = sync_wait(par)

            @pl.when(step < CYCLES * RESTART - 1)
            def _():
                for cp in [x for q in range(3) for x in halo(q, RB.at[c, j, q], h_recv.at[hpar, q])]:
                    cp.wait_send()

            for k in range(RESTART):
                @pl.when(j == k)
                def _():
                    nn = bc(tot, 16 + k)
                    nrm = jnp.sqrt(nn)
                    sg = 1.0 / nrm
                    SIG[k] = sg
                    sig = [SIG[i] for i in range(k)] + [sg]
                    h = [bc(tot, i) * sig[i] * sg for i in range(k + 1)]
                    gcol = [bc(tot, 16 + i) * sig[i] * sg for i in range(k)] + [nn * sg * sg]
                    for i in range(k + 1):
                        GM[i, k] = gcol[i]
                        if i < k:
                            GM[k, i] = gcol[i]
                    if k == 0:
                        beta = MISC[0] * nrm
                        MISC[4] = beta
                        GV[0] = beta
                        RES[c] = jnp.where(lane8 == 0, beta, 0.0)
                    else:
                        est = givens(k - 1, nrm * MISC[3])
                        RES[c] = jnp.where(lane8 == k, est, RES[c])
                    cf = []
                    for i in range(k + 1):
                        gh = gcol[i] * h[k]
                        for m in range(k):
                            gh = gh + GM[i, m] * h[m]
                        cf.append(2.0 * h[i] - gh)
                        RM[i, k] = cf[i]
                    if k == 0:
                        wn = jnp.sqrt(bc(tot, 32)) * sg
                        MISC[3] = wn
                        MISC[2] = 1.0 / wn
                    rho = MISC[2]
                    if k < RESTART - 1:
                        es = [rho * cf[i] * sig[i] for i in range(k + 1)]
                        ew = rho * sg
                        for i in range(k + 1):
                            EC[i] = es[i]
                        EC[k + 1] = ew

                        def body(i, accs):
                            accs = list(accs)
                            for r in range(0, 64, 16):
                                v = [U[m, i, r:r + 16, :].reshape(2, 8, 128) for m in range(k + 1)]
                                u = ew * W[i + 1, LO + r:LO + r + 16, :].reshape(2, 8, 128)
                                for m in range(k + 1):
                                    u = u - es[m] * v[m]
                                for m in range(k + 1):
                                    t = u * v[m]
                                    accs[m] = accs[m] + (t[0] + t[1])
                                t = u * u
                                accs[k + 1] = accs[k + 1] + (t[0] + t[1])
                                u = u.reshape(16, 128)
                                UC[i + 1, LO + r:LO + r + 16, :] = u
                                U[k + 1, i, r:r + 16, :] = u
                            return tuple(accs)

                        accs = lax.fori_loop(0, NP, body, (zero8,) * (k + 2))
                        for i in range(k + 2):
                            ACC[i] = accs[i]
                        seams(UC)
                    else:
                        wn2 = bc(tot, 32) * sg * sg
                        drop = zero8
                        for i in range(k + 1):
                            q = gcol[i] * cf[k]
                            for m in range(k):
                                q = q + GM[i, m] * cf[m]
                            drop = drop + cf[i] * (2.0 * h[i] - q)
                        sub = jnp.sqrt(jnp.maximum(wn2 - drop, 0.0))
                        est = givens(k, sub)
                        RES[c] = jnp.where(lane8 == k + 1, est, RES[c])
                        g = [GV[i] for i in range(RESTART)]
                        for i in reversed(range(RESTART)):
                            y = g[i] / RM[i, i]
                            YY[i] = y * sig[i]
                            for m in range(i):
                                g[m] = g[m] - RM[m, i] * y

        yy = [YY[i] for i in range(RESTART)]

        @pl.when(c == 0)
        def _():
            @pl.loop(0, NP)
            def _(i):
                for r in range(0, 64, 8):
                    x = X[i + 1, LO + r:LO + r + 8, :]
                    for m in range(RESTART):
                        x = x + yy[m] * Z[m, i, r:r + 8, :]
                    X[i + 1, LO + r:LO + r + 8, :] = x

            def ghost_x(rows):
                g = GX[rows, :]
                for m in range(RESTART):
                    g = g + yy[m] * GZ[m, rows, :]
                GX[rows, :] = g
            groups(ghost_x)
            inv = MISC[1]
            ACC[0] = residual(inv)
            for cp in [x for q in range(3) for x in halo(q, RB.at[0, RESTART - 1, q], h_recv.at[1, q])]:
                cp.wait_recv()

            def ghost_r(rows):
                for q in range(3):
                    g = zero8
                    for m in range(RESTART):
                        g = g + yy[m] * RB[0, m, q, rows, :]
                    GU[0, q, rows, :] = GU[0, q, rows, :] - inv * g
            groups(ghost_r)

        @pl.when(c == CYCLES - 1)
        def _():
            @pl.loop(0, NP)
            def _(i):
                x = X[i + 1, LO:HI, :].reshape(8, 8, 128)
                for m in range(RESTART):
                    x = x + yy[m] * Z[m, i].reshape(8, 8, 128)
                x = x.reshape(64, 128)
                out_ref[i] = x[:, 0:64]
                out_ref[i + NP] = x[:, 64:128]

    rows = jnp.where(lax.broadcasted_iota(jnp.int32, (8, 128), 0) == 0, RES[0], RES[1]) * out_scale
    res_ref[...] = rows[0:2, 0:RESTART + 1]


def solution(mesh):
    grid_spec = P(('sys', 'gx'), 'gy', 'gz')
    vel_spec = P(None, ('sys', 'gx'), 'gy', 'gz')
    table_spec = P('sys', None)
    f32 = jnp.float32

    def local_solve(source, initial, velocity, damping):
        big = (NP + 2, ROWS, 128)
        vol = (NP, 64, 128)
        v = lambda *s: pltpu.VMEM(s, f32)
        scratch = [
            v(RESTART, *vol), v(RESTART, *vol),
            v(*big), v(*big), v(*big), v(*big), v(*big), v(*big),
            v(*vol), v(*vol), v(*vol), v(*vol), v(*vol), v(*vol),
            v(RESTART, 3, GROWS, 128), v(CYCLES, RESTART, 3, GROWS, 128), v(3, GROWS, 128),
            v(RESTART, GROWS, 128), v(GROWS, 128),
            v(2, 8, 128), v(RESTART + 1, 8, 128),
            v(RESTART, RESTART, 8, 128), v(RESTART, RESTART, 8, 128),
            v(RESTART, 8, 128), v(RESTART + 1, 8, 128), v(RESTART, 8, 128), v(RESTART, 8, 128),
            v(RESTART + 1, 8, 128), v(RESTART, 8, 128), v(CYCLES, 8, 128), v(8, 8, 128),
            pltpu.SemaphoreType.DMA((8,)), pltpu.SemaphoreType.DMA((2, 8)),
            pltpu.SemaphoreType.DMA((3, 3)), pltpu.SemaphoreType.DMA((2, 3, 3)), pltpu.SemaphoreType.DMA((3,)),
        ]
        vm = pl.BlockSpec(memory_space=pltpu.VMEM)
        return pl.pallas_call(
            kernel,
            out_shape=(jax.ShapeDtypeStruct(source.shape, f32), jax.ShapeDtypeStruct((CYCLES, RESTART + 1), f32)),
            in_specs=[vm, vm, vm, pl.BlockSpec(memory_space=pltpu.SMEM)],
            out_specs=(vm, vm),
            scratch_shapes=scratch,
            compiler_params=pltpu.CompilerParams(
                collective_id=0, has_side_effects=True, vmem_limit_bytes=67043328),
            name='fgmres',
        )(source, initial, velocity, damping)

    return jax.shard_map(local_solve, mesh=mesh, in_specs=(grid_spec, grid_spec, vel_spec, table_spec),
                         out_specs=(grid_spec, table_spec), check_vma=False)
```

time: 5770 us -> 298 us (0.05)
  matrix products: 2370 us -> 0 us
  blocking collectives: 1450 us -> 0 us
  local copies, waits for them, and re-layouts: 736 us -> 3.29 us
  other arithmetic: 677 us -> 0 us
  starting transfers between devices: 358 us -> 0 us
  Pallas kernels: 0 us -> 294 us
  between operations: 149 us -> 0.65 us
    dot_general x74 -> x0, matrix products: 2370 us -> none  [the longest x36 1550 us: local_solve(): jnp.einsum('kabc,abc->k', active, work_vec, preferred_element_type=jnp.fl...]
    psum x62 -> x0, blocking collectives: 1450 us -> none  [the longest x40 903 us: local_solve(): lax.psum(jnp.einsum('kabc,abc->k', active, work_vec, preferred_element_ty...]
    ppermute x132 -> x0, starting transfers between devices: 358 us -> none  [the longest x66 269 us: exchange(): low_plane = lax.ppermute(last_plane, GRID_AXES[axis_pos], to_next)]
    split x294 -> x0, local copies, waits for them, and re-layouts: 353 us -> none  [the longest x186 202 us: stencil(): jnp.split(field, [1], axis=axis_pos)[1]]
    pallas_call x0 -> x1, Pallas kernels: none -> 294 us  [local_solve(): pl.pallas_call(kernel, out_shape=(jax.ShapeDtypeStruct(source.shape, f32)...]
    add x60 -> x0, other arithmetic: 286 us -> none  [the longest x18 158 us: stencil(): result - ahead_val - behind_val]
    scatter x36 -> x0, other arithmetic: 212 us -> none  [the longest x18 118 us: local_solve(): search = search.at[col_id].set(precond_vec)]
    slice x65 -> x0, local copies, waits for them, and re-layouts: 175 us -> none  [the longest x18 145 us: local_solve(): active = basis[:col_id + 1]]
  transfers between devices with their start and end apart: 132 -> 0, of which waited for: 0 -> 0; matrix products, arithmetic and copies ran while one was open for 7% -> 0% of each run, Pallas kernels for 0% -> 0%
where the time goes in v1:
time: 298 us
  Pallas kernels  294 us (99%)
  local copies, waits for them, and re-layouts  3.29 us (1%)
    pallas_call x1, Pallas kernels, local_solve(): pl.pallas_call(kernel, out_shape=(jax.ShapeDtypeStruct(source.shape, f32)...  294 us

profile of v1, /device:TPU:0, one launch (start us, length us, event | category | flops | bytes accessed | tf_op | source)
XLA Modules:
  0.0 297.7 jit_solution(9365627858025472021)
XLA Ops:
  0.6 293.7 %fgmres.1 = (f32[48,64,64]{2,1,0:T(8,128)}, f32[2,11]{1,0:T(2,128)}) custom-call(f32[48,64,64]{2,1,0:T(8,128)} %src_ref.1, f32[48,64,64]{2,1,0:T(8,128)} %ini_ref.1, f32[3,48,64,64]{3,2,1,0:T(8,128)} %vel_ref.1, f32[2,10]{1,0:T(2,128)} %damp_ref.1), custom_call_target="tpu_custom_call" | custom-call | tf_op jit(solution)/shard_map/fgmres/pallas_call | solution.py:511
  294.4 0.0 copy-start
  294.4 2.7 copy.8
  297.1 0.0 copy-done
  297.1 0.6 copy.9
Async XLA Ops:
  294.4 2.7 copy-start

commit v2 on v1

--- a/solution.py
+++ b/solution.py
@@ -13,7 +13,7 @@
 LO, HI, ROWS = 8, 72, 80
 XG, YG, ZG = slice(0, 32), slice(32, 56), slice(56, 120)
 GROWS = 120
-UA, UB, UD, UI, UP, UR, UG = 2, 2, 2, 2, 2, 2, 1
+UA, UB, UD, UI, UP, UR, UG = 24, 24, 24, 24, 24, 4, 5
 
 
 def planes(unroll, body, carry=()):
@@ -39,7 +39,7 @@
 
 def kernel(src_ref, ini_ref, vel_ref, damp_ref, out_ref, res_ref,
            U, Z, UC, ZC, T1, T2, W, X, SRC, CPZ, CMZ, HVX, HVY, CGZ,
-           GU, RB, SB, GZ, GX, SS, ACC, GM, RM, SIG, EC, CS, SN, GV, YY, RES, MISC,
+           GU, RB, SB, GZ, GX, SS, ACC, GM, RM, SIG, EC, CS, SN, GV, YY, NRM, RES, MISC,
            s_send, s_recv, h_send, h_recv, x_recv):
     f32 = jnp.float32
     gx, gy, gz = lax.axis_index('gx'), lax.axis_index('gy'), lax.axis_index('gz')
@@ -313,26 +313,32 @@
             groups(ghost_of_z)
             fill_ghosts(ZC, GZ.at[j])
 
+            cz = GZ[j, ZG, :]
+
+            def apply_a(p, cy):
+                _, az = stencil(ZC, p)
+                W[p, LO:HI, :] = az - ghost_z(cz, p)
+                return cy
+            planes(UD, apply_a)
+
             for k in range(RESTART):
                 @pl.when(j == k)
                 def _():
-                    cz = GZ[k, ZG, :]
-
-                    def one(p, accs):
+                    last = k == 0 or k == RESTART - 1
+
+                    def dots(t, accs):
                         accs = list(accs)
-                        _, az = stencil(ZC, p)
-                        w = az - ghost_z(cz, p)
-                        W[p, LO:HI, :] = w
+                        w = W[pl.ds(t * 2 + 1, 2), LO:HI, :].reshape(16, 8, 128)
                         for i in range(k + 1):
-                            accs[i] = accs[i] + fold(U[i, p - 1] * w)
-                        if k == 0 or k == RESTART - 1:
-                            accs[k + 1] = accs[k + 1] + fold(w * w)
+                            v = U[i, pl.ds(t * 2, 2)].reshape(16, 8, 128)
+                            accs[i] = accs[i] + jnp.sum(v * w, axis=0)
+                        if last:
+                            accs[k + 1] = accs[k + 1] + jnp.sum(w * w, axis=0)
                         return tuple(accs)
-                    accs = planes(UD, one, (zero8,) * (k + 2))
-                    accw = accs[k + 1]
+                    accs = lax.fori_loop(0, NP // 2, dots, (zero8,) * (k + 2 if last else k + 1))
                     items = [(i, accs[i]) for i in range(k + 1)] + [(16 + i, ACC[i]) for i in range(k + 1)]
-                    if k == 0 or k == RESTART - 1:
-                        items.append((32, accw))
+                    if last:
+                        items.append((32, accs[k + 1]))
                     sync_start(par, items)
 
             @pl.when(step < CYCLES * RESTART - 1)
@@ -351,6 +357,12 @@
                 for cp in halo(2, RB.at[c, j, 2], h_recv.at[hpar, 2]):
                     cp.start()
 
+            for k in range(2, RESTART):
+                @pl.when(j == k)
+                def _():
+                    est = givens(k - 2, NRM[k - 1] * MISC[3])
+                    RES[c] = jnp.where(lane8 == k - 1, est, RES[c])
+
             tot = sync_wait(par)
 
             @pl.when(step < CYCLES * RESTART - 1)
@@ -365,76 +377,67 @@
                     nrm = jnp.sqrt(nn)
                     sg = 1.0 / nrm
                     SIG[k] = sg
-                    sig = [SIG[i] for i in range(k)] + [sg]
-                    h = [bc(tot, i) * sig[i] * sg for i in range(k + 1)]
-                    gcol = [bc(tot, 16 + i) * sig[i] * sg for i in range(k)] + [nn * sg * sg]
-                    for i in range(k + 1):
-                        GM[i, k] = gcol[i]
-                        if i < k:
-                            GM[k, i] = gcol[i]
+                    NRM[k] = nrm
+                    sig = SIG[0:k + 1] * sg
+                    h = jnp.stack([bc(tot, i) for i in range(k + 1)]) * sig
+                    gcol = jnp.stack([bc(tot, 16 + i) for i in range(k + 1)]) * sig
+                    GM[k, 0:k + 1] = gcol
+                    if k > 0:
+                        GM[0:k, k] = gcol[0:k]
+
+                    def gram_times(x):
+                        out = gcol * x[k]
+                        for m in range(k):
+                            out = out + GM[m, 0:k + 1] * x[m]
+                        return out
+                    cf = 2.0 * h - gram_times(h)
+                    RM[0:k + 1, k] = cf
                     if k == 0:
                         beta = MISC[0] * nrm
                         MISC[4] = beta
                         GV[0] = beta
                         RES[c] = jnp.where(lane8 == 0, beta, 0.0)
-                    else:
-                        est = givens(k - 1, nrm * MISC[3])
-                        RES[c] = jnp.where(lane8 == k, est, RES[c])
-                    cf = []
-                    for i in range(k + 1):
-                        gh = gcol[i] * h[k]
-                        for m in range(k):
-                            gh = gh + GM[i, m] * h[m]
-                        cf.append(2.0 * h[i] - gh)
-                        RM[i, k] = cf[i]
-                    if k == 0:
                         wn = jnp.sqrt(bc(tot, 32)) * sg
                         MISC[3] = wn
                         MISC[2] = 1.0 / wn
-                    rho = MISC[2]
+                        rho = 1.0 / wn
+                    else:
+                        rho = MISC[2]
                     if k < RESTART - 1:
-                        es = [rho * cf[i] * sig[i] for i in range(k + 1)]
+                        es = rho * cf * SIG[0:k + 1]
                         ew = rho * sg
-                        for i in range(k + 1):
-                            EC[i] = es[i]
+                        EC[0:k + 1] = es
                         EC[k + 1] = ew
 
                         def body(i, accs):
                             accs = list(accs)
-                            for r in range(0, 64, 16):
-                                v = [U[m, i, r:r + 16, :].reshape(2, 8, 128) for m in range(k + 1)]
-                                u = ew * W[i + 1, LO + r:LO + r + 16, :].reshape(2, 8, 128)
+                            for r in range(0, 64, 8):
+                                v = [U[m, i, r:r + 8, :] for m in range(k + 1)]
+                                u = ew * W[i + 1, LO + r:LO + r + 8, :]
                                 for m in range(k + 1):
                                     u = u - es[m] * v[m]
+                                UC[i + 1, LO + r:LO + r + 8, :] = u
+                                U[k + 1, i, r:r + 8, :] = u
                                 for m in range(k + 1):
-                                    t = u * v[m]
-                                    accs[m] = accs[m] + (t[0] + t[1])
-                                t = u * u
-                                accs[k + 1] = accs[k + 1] + (t[0] + t[1])
-                                u = u.reshape(16, 128)
-                                UC[i + 1, LO + r:LO + r + 16, :] = u
-                                U[k + 1, i, r:r + 16, :] = u
+                                    accs[m] = accs[m] + u * v[m]
+                                accs[k + 1] = accs[k + 1] + u * u
                             return tuple(accs)
 
                         accs = lax.fori_loop(0, NP, body, (zero8,) * (k + 2))
-                        for i in range(k + 2):
-                            ACC[i] = accs[i]
+                        ACC[0:k + 2] = jnp.stack(accs)
                         seams(UC)
                     else:
                         wn2 = bc(tot, 32) * sg * sg
-                        drop = zero8
-                        for i in range(k + 1):
-                            q = gcol[i] * cf[k]
-                            for m in range(k):
-                                q = q + GM[i, m] * cf[m]
-                            drop = drop + cf[i] * (2.0 * h[i] - q)
+                        drop = jnp.sum(cf * (2.0 * h - gram_times(cf)), axis=0)
                         sub = jnp.sqrt(jnp.maximum(wn2 - drop, 0.0))
+                        est = givens(k - 1, nrm * MISC[3])
+                        RES[c] = jnp.where(lane8 == k, est, RES[c])
                         est = givens(k, sub)
                         RES[c] = jnp.where(lane8 == k + 1, est, RES[c])
                         g = [GV[i] for i in range(RESTART)]
                         for i in reversed(range(RESTART)):
                             y = g[i] / RM[i, i]
-                            YY[i] = y * sig[i]
+                            YY[i] = y * SIG[i]
                             for m in range(i):
                                 g[m] = g[m] - RM[m, i] * y
 
@@ -503,7 +506,7 @@
             v(2, 8, 128), v(RESTART + 1, 8, 128),
             v(RESTART, RESTART, 8, 128), v(RESTART, RESTART, 8, 128),
             v(RESTART, 8, 128), v(RESTART + 1, 8, 128), v(RESTART, 8, 128), v(RESTART, 8, 128),
-            v(RESTART + 1, 8, 128), v(RESTART, 8, 128), v(CYCLES, 8, 128), v(8, 8, 128),
+            v(RESTART + 1, 8, 128), v(RESTART, 8, 128), v(RESTART, 8, 128), v(CYCLES, 8, 128), v(8, 8, 128),
             pltpu.SemaphoreType.DMA((8,)), pltpu.SemaphoreType.DMA((2, 8)),
             pltpu.SemaphoreType.DMA((3, 3)), pltpu.SemaphoreType.DMA((2, 3, 3)), pltpu.SemaphoreType.DMA((3,)),
         ]

time: 298 us -> 167 us (0.56)
  Pallas kernels: 294 us -> 163 us
    pallas_call x1, Pallas kernels: 294 us -> 163 us  [local_solve(): pl.pallas_call(kernel, out_shape=(jax.ShapeDtypeStruct(source.shape, f32)...]
where the time goes in v2:
time: 167 us
  Pallas kernels  163 us (98%)
  local copies, waits for them, and re-layouts  3.29 us (2%)
    pallas_call x1, Pallas kernels, local_solve(): pl.pallas_call(kernel, out_shape=(jax.ShapeDtypeStruct(source.shape, f32)...  163 us

profile of v2, /device:TPU:0, one launch (start us, length us, event | category | flops | bytes accessed | tf_op | source)
XLA Modules:
  0.0 167.0 jit_solution(3714971591625830591)
XLA Ops:
  0.6 163.0 %fgmres.1 = (f32[48,64,64]{2,1,0:T(8,128)}, f32[2,11]{1,0:T(2,128)}) custom-call(f32[48,64,64]{2,1,0:T(8,128)} %src_ref.1, f32[48,64,64]{2,1,0:T(8,128)} %ini_ref.1, f32[3,48,64,64]{3,2,1,0:T(8,128)} %vel_ref.1, f32[2,10]{1,0:T(2,128)} %damp_ref.1), custom_call_target="tpu_custom_call" | custom-call | tf_op jit(solution)/shard_map/fgmres/pallas_call | solution.py:514
  163.7 0.0 copy-start
  163.7 2.7 %copy.8 = f32[48,64,64]{2,1,0:T(8,128)} copy(f32[48,64,64]{2,1,0:T(8,128)} %get-tuple-element.4) | data formatting | bytes 1572864
  166.4 0.0 copy-done
  166.4 0.6 copy.9
Async XLA Ops:
  163.7 2.7 %copy-start = (f32[2,11]{1,0:T(2,128)S(1)}, f32[2,11]{1,0:T(2,128)}, u32[]{:S(2)}) copy-start(f32[2,11]{1,0:T(2,128)} %get-tuple-element.5) | copy-start | bytes 268

commit v3 on v2

v3 whole, which is shorter than its diff:
```python
import math
import jax
import jax.numpy as jnp
from jax import lax
from jax.experimental import pallas as pl
from jax.experimental.pallas import tpu as pltpu
from jax.sharding import PartitionSpec as P

MESH = pl.DeviceIdType.MESH
RESTART = 10
CYCLES = 2
XL = 12
NP = 2 * XL
PZ = XL + 2
LO, HI, ROWS = 8, 72, 80
XG, YG, ZG = slice(0, 32), slice(32, 56), slice(56, 120)
GROWS = 120
UN, UR, UC_ = 12, 2, 2


def pairs(unroll, body, carry=()):
    if unroll == XL:
        for i in range(XL):
            carry = body(i, carry)
        return carry

    def trip(t, carry):
        for i in range(unroll):
            carry = body(t * unroll + i, carry)
        return carry
    return lax.fori_loop(0, XL // unroll, trip, carry)


def groups(fn):
    def trip(t, carry):
        for i in range(5):
            fn(pl.ds(pl.multiple_of((t * 5 + i) * 8, 8), 8))
        return carry
    lax.fori_loop(0, GROWS // 40, trip, 0)


def v8(x):
    return x.reshape(-1, 8, 128)


def kernel(src_hbm, ini_hbm, vel_hbm, damp_ref, out_hbm, res_ref,
           U, NU, N2U, MU, Z, ZC, W, X, T1, T2, MW, SRC, CZP, CZM, HVX, HVY, CZA,
           GU, RB, SB, GZ, GX, SS, ACC, GM, RM, SIG, EC, CS, SN, GV, YY, NRM, RES, MISC, STG,
           s_send, s_recv, h_send, h_recv, x_recv, l_sem):
    f32 = jnp.float32
    gx, gy, gz = lax.axis_index('gx'), lax.axis_index('gy'), lax.axis_index('gz')
    peers = {}
    for p in range(1, 8):
        a, b, c = p // 4, (p // 2) % 2, p % 2
        peers[p] = {'gx': 1 - gx if a else gx, 'gy': 1 - gy if b else gy, 'gz': 1 - gz if c else gz}
    side = {0: 4, 1: 2, 2: 1}

    loads = [pltpu.make_async_copy(s, STG.at[i], l_sem.at[i]) for i, s in enumerate(
        (ini_hbm, vel_hbm.at[0], vel_hbm.at[1], vel_hbm.at[2], src_hbm))]
    for cp in loads:
        cp.start()
    bar = pltpu.get_barrier_semaphore()
    for p in range(1, 8):
        pl.semaphore_signal(bar, inc=1, device_id=peers[p], device_id_type=MESH)

    lane = lax.broadcasted_iota(jnp.int32, (64, 128), 1)
    lane8 = lane[0:8]
    left = lane < 64
    zh = jnp.where(left, jnp.where(lane < 32, lane, lane - 32), jnp.where(lane < 96, lane - 64, lane - 96))
    first_q, last_q = lane < 32, lane >= 96
    zero64 = jnp.zeros((64, 128), f32)
    zero8 = jnp.zeros((8, 128), f32)
    hi_x = (1 - gx).astype(f32)
    l0 = 31 * (1 - gz)
    o_x = 96 * (1 - gx)
    y_send = HI - 1 - 63 * gy
    y_pad = HI - 65 * gy
    edge_lo = zh == 32 * (1 - gz)
    edge_hi = zh == 31 + 32 * gz

    def seams(V, ghost=None):
        for zl in range(2):
            b = zl * PZ
            a = pltpu.roll(V[b + XL, LO:HI, :], 32, 1)
            d = pltpu.roll(V[b + 1, LO:HI, :], 96, 1)
            lo = 0.0 if ghost is None else ghost[zl] * (1.0 - hi_x)
            hi = 0.0 if ghost is None else ghost[zl] * hi_x
            V[b, LO:HI, :] = jnp.where(first_q, lo, a)
            V[b + XL + 1, LO:HI, :] = jnp.where(last_q, hi, d)

    def neighbours(V, i, ghost=None):
        u0, u1 = V[i + 1, LO:HI, :], V[i + (PZ + 1), LO:HI, :]
        below, above = pltpu.roll(u1, 1, 1), pltpu.roll(u0, 127, 1)
        if ghost is None:
            cm0, cp1 = CZM[i], CZP[i + XL]
        else:
            g = pltpu.roll(ghost, (l0 - i + 128) % 128, 1)
            below = jnp.where(edge_lo, g, below)
            above = jnp.where(edge_hi, g, above)
            cm0, cp1 = CZA[i], CZA[i + XL]
        out = []
        for zl, u, n in ((0, u0, CZP[i] * u1 + cm0 * below), (1, u1, CZM[i + XL] * u0 + cp1 * above)):
            q = i + (zl * PZ + 1)
            yp, ym = V[q, LO + 1:HI + 1, :], V[q, LO - 1:HI - 1, :]
            xp, xm = V[q + 1, LO:HI, :], V[q - 1, LO:HI, :]
            n = n + (xp + xm) - HVX[i + zl * XL] * (xp - xm)
            n = n + (yp + ym) - HVY[i + zl * XL] * (yp - ym)
            out.append((u, n))
        return out

    def fill_ghosts(V, rec):
        g = rec[XG, :]
        full = [jnp.concatenate([pltpu.roll(g, (o_x - 64 * zl - 32 * yh + 128) % 128, 1) for yh in range(2)], axis=0)
                for zl in range(2)]
        seams(V, full)

        def row(i, c):
            for zl in range(2):
                V[i + (zl * PZ + 1), pl.ds(y_pad, 1), :] = rec[pl.ds(i + (32 + zl * XL), 1), :]
            return c
        pairs(XL, row)

    def pack(plane, q):
        pd = (XL - 1) * (1 - gx)
        acc = zero64[0:32]
        for zl in range(2):
            v = plane(zl, pd)
            for yh in range(2):
                slot = 2 * zl + yh
                r = pltpu.roll(v[32 * yh:32 * yh + 32, :], (32 * slot - o_x + 128) % 128, 1)
                here = jnp.logical_and(lane[0:32] >= 32 * slot, lane[0:32] < 32 * slot + 32)
                acc = jnp.where(here, r, acc)
        SB[q, XG, :] = acc

        def row(i, acc):
            for zl in range(2):
                SB[q, pl.ds(i + (32 + zl * XL), 1), :] = plane(zl, i)[pl.ds(y_send - LO, 1), :]
            r = pltpu.roll(plane(1 - gz, i)[...], (i - l0 + 128) % 128, 1)
            return jnp.where(zh == i, r, acc)
        SB[q, ZG, :] = pairs(XL, row, zero64)

    def padded(V):
        return lambda zl, i: V.at[zl * PZ + i + 1, pl.ds(LO, 64), :]

    def dense(V):
        return lambda zl, i: V.at[zl * XL + i]

    def halo(q, dst, recv):
        return [pltpu.make_async_remote_copy(
            src_ref=SB.at[q, rows, :], dst_ref=dst.at[rows, :], send_sem=h_send, recv_sem=recv,
            device_id=peers[side[ax]], device_id_type=MESH) for ax, rows in ((0, XG), (1, YG), (2, ZG))]

    def halo_start(q, dst, recv):
        for cp in halo(q, dst, recv):
            cp.start()

    def halo_all(dst, recv):
        return pltpu.make_async_remote_copy(src_ref=SB, dst_ref=dst, send_sem=h_send, recv_sem=recv,
                                            device_id=peers[1], device_id_type=MESH)

    def sync_all(par):
        return pltpu.make_async_remote_copy(
            src_ref=SS.at[par, pl.ds(1, 7), :], dst_ref=SS.at[par, pl.ds(1, 7), :],
            send_sem=s_send.at[par], recv_sem=s_recv.at[par], device_id=peers[1], device_id_type=MESH)

    def sync_start(par, items):
        row = zero8
        for idx, acc in items:
            row = jnp.where(lane8 == idx, jnp.sum(acc, axis=1, keepdims=True), row)
        row = row + pltpu.roll(row, 4, 0)
        row = row + pltpu.roll(row, 2, 0)
        row = row + pltpu.roll(row, 1, 0)
        SS[par, 0:1, :] = row[0:1]
        for p in range(1, 8):
            pltpu.make_async_remote_copy(
                src_ref=SS.at[par, pl.ds(0, 1), :], dst_ref=SS.at[par, pl.ds(p, 1), :],
                send_sem=s_send.at[par], recv_sem=s_recv.at[par],
                device_id=peers[p], device_id_type=MESH).start()

    def sync_wait(par):
        sync_all(par).wait_recv()
        tot = SS[par]
        tot = tot + pltpu.roll(tot, 4, 0)
        tot = tot + pltpu.roll(tot, 2, 0)
        return tot + pltpu.roll(tot, 1, 0)

    def bc(tot, k):
        return jnp.broadcast_to(tot[:, k:k + 1], (8, 128))

    def fold(x):
        return jnp.sum(v8(x), axis=0)

    def poly(c, j):
        s = damp_ref[c, j] / 6.0
        a0, a1, a2 = 3.0 * s, 3.0 * s * s, s * s * s
        return a0 - 6.0 * a1 + 36.0 * a2, a1 - 12.0 * a2, a2

    @pl.loop(0, 2 * PZ)
    def _(p):
        for V in (ZC, W, X, T1.at[0], T1.at[1]):
            V[p, 0:LO, :] = zero8
            V[p, HI:ROWS, :] = zero8

    odd = jnp.where(left, 0, 1)
    pos = jnp.where(left, lane, lane - 64)
    deal = jnp.where(pos < 32, 2 * pos, 2 * pos) + odd

    def convert(ref, i):
        both = []
        for h in (0, 2):
            a = jnp.concatenate([ref[h * XL + i], ref[(h + 1) * XL + i]], axis=1)
            both.append(jnp.take_along_axis(a, deal, axis=1))
        p01, p23 = both
        return (jnp.where(left, p01, pltpu.roll(p23, 64, 1)), jnp.where(left, pltpu.roll(p01, 64, 1), p23))

    loads[0].wait()

    def load_x(i, c):
        for zl, v in enumerate(convert(STG.at[0], i)):
            X[i + (zl * PZ + 1), LO:HI, :] = v
        return c
    pairs(UC_, load_x)
    pack(padded(X), 0)
    pl.semaphore_wait(bar, 7)
    halo_start(0, GX, x_recv)
    for cp in loads[1:]:
        cp.wait()

    def load_rest(i, c):
        hx, hy, hz, sv = (convert(STG.at[q], i) for q in range(1, 5))
        for zl in range(2):
            r = i + zl * XL
            HVX[r] = 0.5 * hx[zl]
            HVY[r] = 0.5 * hy[zl]
            SRC[r] = sv[zl]
        cm0, cp1 = 1.0 + 0.5 * hz[0], 1.0 - 0.5 * hz[1]
        CZP[i] = 1.0 - 0.5 * hz[0]
        CZM[i] = jnp.where(zh == 0, 0.0, cm0)
        CZA[i] = jnp.where(zh == 32 * gz, 0.0, cm0)
        CZM[i + XL] = 1.0 + 0.5 * hz[1]
        CZP[i + XL] = jnp.where(zh == 31, 0.0, cp1)
        CZA[i + XL] = jnp.where(zh == 63 - 32 * gz, 0.0, cp1)
        return c
    pairs(UC_, load_rest)
    for cp in halo(0, GX, x_recv):
        cp.wait_send()
    pltpu.make_async_remote_copy(src_ref=SB.at[0], dst_ref=GX, send_sem=h_send, recv_sem=x_recv,
                                 device_id=peers[1], device_id_type=MESH).wait_recv()

    def residual(scale):
        fill_ghosts(X, GX)
        cz = GX[ZG, :]

        def one(i, acc):
            for zl, (u, n) in enumerate(neighbours(X, i, cz)):
                r = SRC[i + zl * XL] - (6.0 * u - n)
                if scale is not None:
                    r = (v8(r) * scale).reshape(64, 128)
                    U[0, i + zl * XL] = r
                W[i + (zl * PZ + 1), LO:HI, :] = r
                acc = acc + fold(r * r)
            return acc
        acc = pairs(UR, one, zero8)
        seams(W)
        return acc

    def apply_n(V, store, unroll):
        def one(i, c):
            for zl, (u, n) in enumerate(neighbours(V, i)):
                store(zl, i, u, n)
            return c
        pairs(unroll, one)

    def to_t1(b):
        def store(zl, i, u, n):
            T1[b, i + (zl * PZ + 1), LO:HI, :] = n
        return store

    def ghosts_of_z(k, q):
        def one(rows):
            GZ[k, rows, :] = q[0] * GU[k, 0, rows, :] + q[1] * GU[k, 1, rows, :] + q[2] * GU[k, 2, rows, :]
        groups(one)
        fill_ghosts(ZC, GZ.at[k])

    acc0 = residual(None)
    sync_start(0, [(16, acc0)])
    pack(padded(W), 0)
    halo_start(0, GU.at[0, 0], h_recv.at[1])
    apply_n(W, to_t1(0), UR)
    seams(T1.at[0])
    pack(padded(T1.at[0]), 1)
    halo_start(1, GU.at[0, 1], h_recv.at[1])

    def to_t2(zl, i, u, n):
        T2[0, i + zl * XL] = n
    apply_n(T1.at[0], to_t2, UR)
    pack(dense(T2.at[0]), 2)
    halo_start(2, GU.at[0, 2], h_recv.at[1])
    tot = sync_wait(0)
    sync_all(0).wait_send()
    beta0 = jnp.sqrt(bc(tot, 16))
    inv0 = 1.0 / beta0
    MISC[0] = beta0
    MISC[1] = inv0
    ACC[0] = acc0 * inv0 * inv0
    q0 = poly(0, 0)

    def scale_start(i, c):
        for zl in range(2):
            r = i + zl * XL
            u = (v8(W[i + (zl * PZ + 1), LO:HI, :]) * inv0).reshape(64, 128)
            n = (v8(T1[0, i + (zl * PZ + 1), LO:HI, :]) * inv0).reshape(64, 128)
            n2 = (v8(T2[0, r]) * inv0).reshape(64, 128)
            U[0, r] = u
            NU[0, r] = n
            N2U[0, r] = n2
            z = q0[0] * u + q0[1] * n + q0[2] * n2
            Z[0, r] = z
            ZC[i + (zl * PZ + 1), LO:HI, :] = z
        return c
    pairs(UR, scale_start)
    halo_all(GU.at[0], h_recv.at[1]).wait_recv()
    halo_all(GU.at[0], h_recv.at[1]).wait_send()

    def rescale_ghost(rows):
        for q in range(3):
            GU[0, q, rows, :] = GU[0, q, rows, :] * inv0
    groups(rescale_ghost)
    ghosts_of_z(0, q0)

    def givens(m, sub):
        h = [RM[i, m] for i in range(m + 1)]
        for i in range(m):
            cs, sn = CS[i], SN[i]
            h[i], h[i + 1] = cs * h[i] + sn * h[i + 1], cs * h[i + 1] - sn * h[i]
        d = h[m]
        rad = jnp.sqrt(d * d + sub * sub)
        cs, sn = d / rad, sub / rad
        CS[m] = cs
        SN[m] = sn
        h[m] = cs * d + sn * sub
        RM[0:m + 1, m] = jnp.stack(h)
        g = GV[m]
        GV[m] = cs * g
        GV[m + 1] = -sn * g
        est = MISC[4] * jnp.abs(sn)
        MISC[4] = est
        return est

    out_scale = 1.0 / math.sqrt(1572864.0)

    @pl.loop(0, CYCLES)
    def _(c):
        @pl.loop(0, RESTART)
        def _(j):
            step = c * RESTART + j
            par = (step + 1) % 2
            b = step % 2
            nxt = (j + 1) % RESTART
            slot = c * RESTART + (1 - c) * j + c * (j % 2)

            cz = GZ[j, ZG, :]

            def apply_a(i, cy):
                for zl, (u, n) in enumerate(neighbours(ZC, i, cz)):
                    W[i + (zl * PZ + 1), LO:HI, :] = 6.0 * u - n
                return cy
            pairs(UN, apply_a)

            for k in range(RESTART):
                @pl.when(j == k)
                def _():
                    ends = k == 0 or k == RESTART - 1
                    accs = (zero8,) * (k + 2 if ends else k + 1)

                    def dots(t, accs):
                        accs = list(accs)
                        w = W[pl.ds(t * 2 + 2 * (t // (XL // 2)) + 1, 2), LO:HI, :].reshape(16, 8, 128)
                        for i in range(k + 1):
                            v = U[i, pl.ds(t * 2, 2)].reshape(16, 8, 128)
                            accs[i] = accs[i] + jnp.sum(v * w, axis=0)
                        if ends:
                            accs[k + 1] = accs[k + 1] + jnp.sum(w * w, axis=0)
                        return tuple(accs)
                    accs = lax.fori_loop(0, XL, dots, accs)
                    items = [(i, accs[i]) for i in range(k + 1)] + [(16 + i, ACC[i]) for i in range(k + 1)]
                    if ends:
                        items.append((32, accs[k + 1]))
                    sync_start(par, items)

            @pl.when(step < CYCLES * RESTART - 1)
            def _():
                seams(W)
                pack(padded(W), 0)
                halo_start(0, RB.at[slot, 0], h_recv.at[b])
                apply_n(W, to_t1(b), UN)
                seams(T1.at[b])
                pack(padded(T1.at[b]), 1)
                halo_start(1, RB.at[slot, 1], h_recv.at[b])
                q0, q1, q2 = poly(c, nxt)

                def store(zl, i, u, n):
                    r = i + zl * XL
                    T2[b, r] = n
                    MW[r] = q0 * W[i + (zl * PZ + 1), LO:HI, :] + q1 * u + q2 * n
                apply_n(T1.at[b], store, UN)
                pack(dense(T2.at[b]), 2)
                halo_start(2, RB.at[slot, 2], h_recv.at[b])

            for k in range(RESTART):
                @pl.when(j == k)
                def _():
                    if k < RESTART - 1:
                        q0, q1, q2 = poly(c, k + 1)
                        e = [EC[i] for i in range(k + 1)] if k else None

                        def body(r, cy):
                            if k:
                                n = e[k] * v8(T1[1 - b, r + 2 * (r // XL) + 1, LO:HI, :])
                                n2 = e[k] * v8(T2[1 - b, r])
                                for m in range(k):
                                    nm, n2m = v8(NU[m, r]), v8(N2U[m, r])
                                    n = n - e[m] * nm
                                    n2 = n2 - e[m] * n2m
                                    MU[m, r] = (q0 * v8(U[m, r]) + q1 * nm + q2 * n2m).reshape(64, 128)
                                NU[k, r] = n.reshape(64, 128)
                                N2U[k, r] = n2.reshape(64, 128)
                            else:
                                n, n2 = v8(NU[0, r]), v8(N2U[0, r])
                            MU[k, r] = (q0 * v8(U[k, r]) + q1 * n + q2 * n2).reshape(64, 128)
                            return cy
                        lax.fori_loop(0, NP, body, 0)
                    if k >= 2:
                        est = givens(k - 2, NRM[k - 1] * MISC[3])
                        RES[c] = jnp.where(lane8 == k - 1, est, RES[c])

            tot = sync_wait(par)

            for k in range(RESTART):
                @pl.when(j == k)
                def _():
                    nn = bc(tot, 16 + k)
                    nrm = jnp.sqrt(nn)
                    sg = 1.0 / nrm
                    SIG[k] = sg
                    NRM[k] = nrm
                    sig = SIG[0:k + 1] * sg
                    h = jnp.stack([bc(tot, i) for i in range(k + 1)]) * sig
                    gcol = jnp.stack([bc(tot, 16 + i) for i in range(k + 1)]) * sig
                    GM[k, 0:k + 1] = gcol
                    if k > 0:
                        GM[0:k, k] = gcol[0:k]

                    def gram_times(x):
                        out = gcol * x[k]
                        for m in range(k):
                            out = out + GM[m, 0:k + 1] * x[m]
                        return out
                    cf = 2.0 * h - gram_times(h)
                    RM[0:k + 1, k] = cf
                    if k == 0:
                        beta = MISC[0] * nrm
                        MISC[4] = beta
                        GV[0] = beta
                        RES[c] = jnp.where(lane8 == 0, beta, 0.0)
                        wn = jnp.sqrt(bc(tot, 32)) * sg
                        MISC[3] = wn
                        rho = 1.0 / wn
                        MISC[2] = rho
                    else:
                        rho = MISC[2]
                    if k < RESTART - 1:
                        es = rho * cf * SIG[0:k + 1]
                        ew = rho * sg
                        EC[0:k + 1] = es
                        EC[k + 1] = ew

                        def body(r, accs):
                            accs = list(accs)
                            q = r + 2 * (r // XL) + 1
                            for y in range(0, 64, 16):
                                v = [v8(U[m, r, y:y + 16, :]) for m in range(k + 1)]
                                u = ew * v8(W[q, LO + y:LO + y + 16, :])
                                z = ew * v8(MW[r, y:y + 16, :])
                                for m in range(k + 1):
                                    u = u - es[m] * v[m]
                                    z = z - es[m] * v8(MU[m, r, y:y + 16, :])
                                U[k + 1, r, y:y + 16, :] = u.reshape(16, 128)
                                z = z.reshape(16, 128)
                                Z[k + 1, r, y:y + 16, :] = z
                                ZC[q, LO + y:LO + y + 16, :] = z
                                for m in range(k + 1):
                                    accs[m] = accs[m] + jnp.sum(u * v[m], axis=0)
                                accs[k + 1] = accs[k + 1] + jnp.sum(u * u, axis=0)
                            return tuple(accs)
                        accs = lax.fori_loop(0, NP, body, (zero8,) * (k + 2))
                        ACC[0:k + 2] = jnp.stack(accs)

                        halo_all(RB.at[slot], h_recv.at[b]).wait_recv()

                        def ghost_u(rows):
                            for q in range(3):
                                g = ew * RB[slot, q, rows, :]
                                for i in range(k + 1):
                                    g = g - es[i] * GU[i, q, rows, :]
                                GU[k + 1, q, rows, :] = g
                        groups(ghost_u)
                    else:
                        wn2 = bc(tot, 32) * sg * sg
                        drop = jnp.sum(cf * (2.0 * h - gram_times(cf)), axis=0)
                        sub = jnp.sqrt(jnp.maximum(wn2 - drop, 0.0))
                        est = givens(k - 1, nrm * MISC[3])
                        RES[c] = jnp.where(lane8 == k, est, RES[c])
                        est = givens(k, sub)
                        RES[c] = jnp.where(lane8 == k + 1, est, RES[c])
                        g = [GV[i] for i in range(RESTART)]
                        for i in reversed(range(RESTART)):
                            y = g[i] / RM[i, i]
                            YY[i] = y * SIG[i]
                            for m in range(i):
                                g[m] = g[m] - RM[m, i] * y

            @pl.when(j < RESTART - 1)
            def _():
                ghosts_of_z(nxt, poly(c, nxt))
            sync_all(par).wait_send()

            @pl.when(step < CYCLES * RESTART - 1)
            def _():
                halo_all(RB.at[slot], h_recv.at[b]).wait_send()

        yy = [YY[i] for i in range(RESTART)]

        @pl.when(c == 0)
        def _():
            def update(i, cy):
                for zl in range(2):
                    q, r = i + (zl * PZ + 1), i + zl * XL
                    x = v8(X[q, LO:HI, :])
                    for m in range(RESTART):
                        x = x + yy[m] * v8(Z[m, r])
                    X[q, LO:HI, :] = x.reshape(64, 128)
                return cy
            pairs(1, update)

            def ghost_x(rows):
                g = GX[rows, :]
                for m in range(RESTART):
                    g = g + yy[m] * GZ[m, rows, :]
                GX[rows, :] = g
            groups(ghost_x)
            inv = MISC[1]
            ACC[0] = residual(inv)
            halo_all(RB.at[RESTART - 1], h_recv.at[1]).wait_recv()

            def ghost_r(rows):
                for q in range(3):
                    g = zero8
                    for m in range(RESTART):
                        g = g + yy[m] * RB[m, q, rows, :]
                    GU[0, q, rows, :] = GU[0, q, rows, :] - inv * g
            groups(ghost_r)

            apply_n(W, to_t1(0), UR)
            seams(T1.at[0])
            q0, q1, q2 = poly(1, 0)

            def first_z(zl, i, u, n):
                r = i + zl * XL
                NU[0, r] = u
                N2U[0, r] = n
                z = q0 * U[0, r] + q1 * u + q2 * n
                Z[0, r] = z
                ZC[i + (zl * PZ + 1), LO:HI, :] = z
            apply_n(T1.at[0], first_z, UR)
            ghosts_of_z(0, (q0, q1, q2))

        @pl.when(c == CYCLES - 1)
        def _():
            def update(i, cy):
                for zl in range(2):
                    q, r = i + (zl * PZ + 1), i + zl * XL
                    x = v8(X[q, LO:HI, :])
                    for m in range(RESTART):
                        x = x + yy[m] * v8(Z[m, r])
                    SRC[r] = x.reshape(64, 128)
                return cy
            pairs(1, update)

    cp = pltpu.make_async_copy(SRC, out_hbm, l_sem.at[0])
    cp.start()
    rows = jnp.where(lax.broadcasted_iota(jnp.int32, (8, 128), 0) == 0, RES[0], RES[1]) * out_scale
    res_ref[...] = rows
    cp.wait()


def unpack(x_ref, r_ref, out_ref, res_ref):
    lane = lax.broadcasted_iota(jnp.int32, (64, 128), 1)
    left = lane < 64
    z = jnp.where(left, lane, lane - 64)
    half = lax.shift_right_logical(z, 1)
    deal = half + 64 * (z - 2 * half) + jnp.where(left, 0, 32)
    for i in range(x_ref.shape[1]):
        e, o = x_ref[0, i], x_ref[1, i]
        for h, p in ((0, jnp.where(left, e, pltpu.roll(o, 64, 1))), (2, jnp.where(left, pltpu.roll(e, 64, 1), o))):
            a = jnp.take_along_axis(p, deal, axis=1)
            out_ref[h, i] = a[:, 0:64]
            out_ref[h + 1, i] = a[:, 64:128]
    res_ref[...] = r_ref[0:CYCLES, 0:RESTART + 1]


def solution(mesh):
    grid_spec = P(('sys', 'gx'), 'gy', 'gz')
    vel_spec = P(None, ('sys', 'gx'), 'gy', 'gz')
    table_spec = P('sys', None)
    f32 = jnp.float32

    def local_solve(source, initial, velocity, damping):
        big = (2 * PZ, ROWS, 128)
        vol = (NP, 64, 128)
        v = lambda *s: pltpu.VMEM(s, f32)
        n = RESTART
        scratch = [
            v(n, *vol), v(n - 1, *vol), v(n - 1, *vol), v(n - 1, *vol), v(n, *vol),
            v(*big), v(*big), v(*big), v(2, *big), v(2, *vol), v(*vol),
            v(*vol), v(*vol), v(*vol), v(*vol), v(*vol), v(*vol),
            v(n, 3, GROWS, 128), v(n + 2, 3, GROWS, 128), v(3, GROWS, 128), v(n, GROWS, 128), v(GROWS, 128),
            v(2, 8, 128), v(n + 1, 8, 128), v(n, n, 8, 128), v(n, n, 8, 128),
            v(n, 8, 128), v(n + 1, 8, 128), v(n, 8, 128), v(n, 8, 128), v(n + 1, 8, 128), v(n, 8, 128), v(n, 8, 128),
            v(CYCLES, 8, 128), v(8, 8, 128), v(5, 48, 64, 64),
            pltpu.SemaphoreType.DMA((2,)), pltpu.SemaphoreType.DMA((2,)), pltpu.SemaphoreType.DMA,
            pltpu.SemaphoreType.DMA((2,)), pltpu.SemaphoreType.DMA, pltpu.SemaphoreType.DMA((5,)),
        ]
        hbm = pl.BlockSpec(memory_space=pl.ANY)
        packed, rows = pl.pallas_call(
            kernel,
            out_shape=(jax.ShapeDtypeStruct(vol, f32), jax.ShapeDtypeStruct((8, 128), f32)),
            in_specs=[hbm, hbm, hbm, pl.BlockSpec(memory_space=pltpu.SMEM)],
            out_specs=(hbm, pl.BlockSpec(memory_space=pltpu.VMEM)),
            scratch_shapes=scratch,
            compiler_params=pltpu.CompilerParams(
                collective_id=0, has_side_effects=True, vmem_limit_bytes=67043328),
            name='fgmres',
        )(source, initial, velocity, damping)
        step = 3
        out, res = pl.pallas_call(
            unpack,
            grid=(XL // step,),
            out_shape=(jax.ShapeDtypeStruct((4, XL, 64, 64), f32), jax.ShapeDtypeStruct((CYCLES, n + 1), f32)),
            in_specs=[pl.BlockSpec((2, step, 64, 128), lambda i: (0, i, 0, 0)), pl.BlockSpec((8, 128), lambda i: (0, 0))],
            out_specs=(pl.BlockSpec((4, step, 64, 64), lambda i: (0, i, 0, 0)),
                       pl.BlockSpec((CYCLES, n + 1), lambda i: (0, 0))),
            name='unpack',
        )(packed.reshape(2, XL, 64, 128), rows)
        return out.reshape(source.shape), res

    return jax.shard_map(local_solve, mesh=mesh, in_specs=(grid_spec, grid_spec, vel_spec, table_spec),
                         out_specs=(grid_spec, table_spec), check_vma=False)
```

time: 167 us -> 157 us (0.940)
  Pallas kernels: 163 us -> 156 us
  local copies, waits for them, and re-layouts: 3.29 us -> 0 us
    pallas_call x1 -> x2, Pallas kernels: 163 us -> 156 us  [the longest x1 152 us: local_solve(): pl.pallas_call(kernel, out_shape=(jax.ShapeDtypeStruct(vol, f32), jax.Sha...]
    unnamed x4 -> x0, local copies, waits for them, and re-layouts: 3.29 us -> none
where the time goes in v3:
time: 157 us; the launch traced here: 156 us
  Pallas kernels  156 us (99%)
    pallas_call x1, Pallas kernels, local_solve(): pl.pallas_call(kernel, out_shape=(jax.ShapeDtypeStruct(vol, f32), jax.Sha...  152 us
    pallas_call x1, Pallas kernels, local_solve(): pl.pallas_call(unpack, grid=(XL // step,), out_shape=(jax.ShapeDtypeStruc...  3.99 us

profile of v3, /device:TPU:0, one launch (start us, length us, event | category | flops | bytes accessed | tf_op | source)
XLA Modules:
  0.0 156.4 jit_solution(3422838617199130626)
XLA Ops:
  0.6 151.7 %fgmres.1 = (f32[24,64,128]{2,1,0:T(8,128)}, f32[8,128]{1,0:T(8,128)}) custom-call(f32[48,64,64]{2,1,0:T(8,128)} %src_hbm.1, f32[48,64,64]{2,1,0:T(8,128)} %ini_hbm.1, f32[3,48,64,64]{3,2,1,0:T(8,128)} %vel_hbm.1, f32[2,10]{1,0:T(2,128)} %damp_ref.1), custom_call_target="tpu_custom_call" | custom-call | tf_op jit(solution)/shard_map/fgmres/pallas_call | solution.py:635
  152.4 4.0 %unpack.1 = (f32[4,12,64,64]{3,2,1,0:T(8,128)}, f32[2,11]{1,0:T(2,128)}) custom-call(f32[2,12,64,128]{3,2,1,0:T(8,128)} %bitcast.2, f32[8,128]{1,0:T(8,128)} %get-tuple-element.7.r_ref), custom_call_target="tpu_custom_call" | custom-call | tf_op jit(solution)/shard_map/unpack/pallas_call | solution.py:646
